TPU v7x, 512 devices: a whole 4x4x16 slice. The times are simulated.
512 devices in a mesh: hot: 32 (over y, x, core), tt: 16 (over z).
Axes of the slice: x: 4, y: 4, z: 16, core: 2. Of those that a mesh axis runs over, the one named last changes fastest.
Arguments:
- hot_table: float32 [8192, 256], P('hot'), may hold values from -1.5 to 1.5
- hot_accum: float32 [8192], P('hot'), may hold values from 0.05 to 1
- hot_owner: int32 [131072, 1], P(('hot', 'tt')), may hold values from 0 to 31; in each aligned block of 256 rows (0 to 255, 256 to 511, ...) at most 16 rows name the same one
- hot_row: int32 [512, 256], P(('hot', 'tt')), may hold values from 0 to 255
- hot_bag: int32 [512, 256], P(('hot', 'tt')), may hold values from 0 to 63, never falling along the last dimension, each value on 1 to 12 neighbouring positions
- cold_owner: int32 [262144, 1], P(('hot', 'tt')), may hold values from 0 to 15; in each aligned block of 512 rows (0 to 511, 512 to 1023, ...) at most 64 rows name the same one
- first_index: int32 [512, 512], P(('hot', 'tt')), may hold values from 0 to 127
- mid_index: int32 [512, 512], P(('hot', 'tt')), may hold values from 0 to 63
- last_index: int32 [512, 512], P(('hot', 'tt')), may hold values from 0 to 63
- cold_bag: int32 [512, 512], P(('hot', 'tt')), may hold values from 0 to 63, never falling along the last dimension, each value on 1 to 24 neighbouring positions
- core_first: float32 [2048, 256], P('tt'), may hold values from -1 to 1
- core_mid: bfloat16 [64, 8192], replicated, may hold values from -1 to 1
- core_last: bfloat16 [64, 128], replicated, may hold values from -6 to 6
- bag_grads: bfloat16 [32768, 256], P(('hot', 'tt')), may hold values from -6 to 6
Outputs:
- pooled: float32 [32768, 256], P(('hot', 'tt'))
- new_table: float32 [8192, 256], P('hot')
- new_accum: float32 [8192], P('hot')
- new_first: float32 [2048, 256], P('tt')
Inputs may be any that keep to these rules, and one draw needn't show every extreme that they name: `hot_owner`: among the 256 hot lookups of one device no owner appears more than 16 times; some owner appears exactly that often. `cold_owner`: among the 512 cold lookups of one device no owner appears more than 64 times; some owner appears exactly that often. `hot_bag`: never falling along a device's lookups; every bag of a device has at least one hot lookup. `cold_bag`: never falling along a device's lookups; every bag of a device has at least one cold lookup.
All inputs are finite; a program needn't handle non-finite values.
Results may differ from a plain program's by a relative error of at most 0.005.
Values may be sent and summed in bfloat16 or wider, within the bound.
A program may use at most 64 MiB of HBM per device.

v0:
```python
import math

import jax
import jax.numpy as jnp
from jax import lax
from jax.sharding import PartitionSpec as P

E1 = 8
E2 = 8
E3 = 4
RANK = 32


def in_blocks(shard, dim, devices):
    dims = shard.shape
    tiles = shard.reshape(*dims[:dim], devices, dims[dim] // devices, *dims[dim + 1 :])
    return jnp.moveaxis(tiles, dim, 0)


def sum_at_owner(shard, axis, dim):
    tiles = in_blocks(shard, dim, lax.axis_size(axis))
    arrived = lax.all_to_all(tiles, axis, split_axis=0, concat_axis=0, tiled=True)
    return arrived.sum(axis=0)


def in_one_piece(arrays, axis, dim, along):
    widths = [math.prod(a.shape[along:]) for a in arrays]
    both = jnp.concatenate(
        [a.reshape(*a.shape[:along], w) for a, w in zip(arrays, widths)], axis=along
    )
    result = lax.all_gather(both, axis, axis=dim, tiled=True)
    tiles = jnp.split(result, [sum(widths[:k]) for k in range(1, len(widths))], axis=along)
    return tuple(
        (b.reshape(*result.shape[:along], *a.shape[along:]) for a, b in zip(arrays, tiles))
    )


def gathered_total(shard, axis):
    return lax.all_gather(shard, axis).sum(0)


def slots_of(owners, peer_count):
    chosen = (owners[:, None] == jnp.arange(peer_count, dtype=jnp.int32)[None, :]).astype(jnp.int32)
    before = jnp.cumsum(chosen, axis=0) - chosen
    return jnp.sum(before * chosen, axis=1)


def slot_source(slot_keys, total_slots):
    lookups = slot_keys.shape[0]
    empty = jnp.full((total_slots,), lookups, jnp.int32)
    return empty.at[slot_keys].set(jnp.arange(lookups, dtype=jnp.int32))


def packed(values, source, fill_value):
    return jnp.take(values, source, axis=0, mode="fill", fill_value=fill_value)


def owner_sum(targets, values, held, precision):
    block_rows = math.gcd(held, 512)
    starts = jnp.arange(held // block_rows, dtype=jnp.int32) * block_rows
    offsets = jnp.arange(block_rows, dtype=jnp.int32)

    def owner_one_block(start):
        picks = ((start + offsets)[:, None] == targets[None, :]).astype(values.dtype)
        return jnp.dot(picks, values, precision=precision, preferred_element_type=jnp.float32)

    return lax.map(owner_one_block, starts).reshape(held, values.shape[1])


def adagrad(table_part, accum_part, grad_part):
    accum_next = accum_part + jnp.mean(grad_part * grad_part, axis=1)
    return (table_part - 0.1 * grad_part / (jnp.sqrt(accum_next)[:, None] + 1e-08), accum_next)


def rank_maps(core_mid, core_last, middle, lasts):
    lookups = middle.shape[0]
    block_rows = math.gcd(lookups, 128)

    def rank_one_block(indices):
        mid_part, last_part = indices
        mid_cores = core_mid[mid_part].reshape(-1, RANK, E2, RANK)
        last_cores = core_last[last_part].reshape(-1, RANK, E3)
        made = jnp.einsum(
            "nawb,nbe->nawe", mid_cores, last_cores, preferred_element_type=jnp.float32
        )
        return made.astype(jnp.bfloat16).reshape(-1, RANK * E2 * E3)

    blocks = lax.map(
        rank_one_block, (middle.reshape(-1, block_rows), lasts.reshape(-1, block_rows))
    )
    return blocks.reshape(lookups, RANK * E2 * E3)


def local(
    hot_table,
    hot_accum,
    hot_owner,
    hot_row,
    hot_bag,
    cold_owner,
    first_index,
    mid_index,
    last_index,
    cold_bag,
    core_first,
    core_mid,
    core_last,
    bag_grads,
):
    rows_held = hot_table.shape[0]
    feature_width = hot_table.shape[1]
    tail_width = feature_width // E1
    bag_count = bag_grads.shape[0]
    bag_range = jnp.arange(bag_count, dtype=jnp.int32)
    hot_peers = lax.axis_size("hot")
    hot_lookups = hot_owner.shape[0]
    hot_cap = 2 * hot_lookups // hot_peers
    row_owner = hot_owner[:, 0]
    row_key = row_owner * hot_cap + slots_of(row_owner, hot_peers)
    row_source = slot_source(row_key, hot_peers * hot_cap)
    request = packed(hot_row[0], row_source, -1).reshape(hot_peers, hot_cap)
    wanted = lax.all_to_all(request, "hot", split_axis=0, concat_axis=0, tiled=True)
    picked = hot_table[jnp.maximum(wanted, 0)].astype(jnp.bfloat16)
    replies = lax.all_to_all(picked, "hot", split_axis=0, concat_axis=0, tiled=True)
    served = wanted
    hot_rows = replies.reshape(-1, feature_width)[row_key]
    hot_pick = (hot_bag[0][:, None] == bag_range[None, :]).astype(jnp.bfloat16)
    hot_cot = jnp.dot(hot_pick, bag_grads, preferred_element_type=jnp.float32).astype(jnp.bfloat16)
    sending = packed(hot_cot, row_source, 0).reshape(hot_peers, hot_cap, feature_width)
    received = lax.all_to_all(sending, "hot", split_axis=0, concat_axis=0, tiled=True)
    row_grad = owner_sum(served.reshape(-1), received.reshape(-1, feature_width), rows_held, None)
    share_grad = sum_at_owner(row_grad, "tt", 0)
    share_rows = share_grad.shape[0]
    share_start = lax.axis_index("tt") * share_rows
    table_share = lax.dynamic_slice_in_dim(hot_table, share_start, share_rows, 0)
    accum_share = lax.dynamic_slice_in_dim(hot_accum, share_start, share_rows, 0)
    table_next, accum_next = adagrad(table_share, accum_share, share_grad)
    new_table, new_accum = in_one_piece((table_next, accum_next), "tt", 0, 1)
    slices_held = core_first.shape[0]
    tt_peers = lax.axis_size("tt")
    cold_lookups = cold_owner.shape[0]
    cold_cap = 2 * cold_lookups // tt_peers
    slice_owner = cold_owner[:, 0]
    slice_key = slice_owner * cold_cap + slots_of(slice_owner, tt_peers)
    slice_source = slot_source(slice_key, tt_peers * cold_cap)
    maps = rank_maps(core_mid, core_last, mid_index[0], last_index[0])
    cold_pick = (cold_bag[0][:, None] == bag_range[None, :]).astype(jnp.bfloat16)
    cold_cot = jnp.dot(cold_pick, bag_grads, preferred_element_type=jnp.float32).astype(
        jnp.bfloat16
    )
    slice_request = packed(first_index[0], slice_source, -1).reshape(tt_peers, cold_cap)
    wanted = lax.all_to_all(slice_request, "tt", split_axis=0, concat_axis=0, tiled=True)
    slices = core_first[jnp.maximum(wanted, 0)].astype(jnp.bfloat16)
    back = lax.all_to_all(slices, "tt", split_axis=0, concat_axis=0, tiled=True)
    slices = back.reshape(-1, E1 * RANK)[slice_key].reshape(cold_lookups, E1, RANK)
    maps_three = maps.reshape(cold_lookups, RANK, tail_width)
    cold_rows = jnp.einsum("kea,kaj->kej", slices, maps_three, preferred_element_type=jnp.float32)
    cold_rows = cold_rows.astype(jnp.bfloat16).reshape(cold_lookups, feature_width)
    local_terms = jnp.einsum(
        "kej,kaj->kea",
        cold_cot.reshape(cold_lookups, E1, tail_width),
        maps_three,
        preferred_element_type=jnp.float32,
    )
    grad_out = packed(local_terms.reshape(cold_lookups, E1 * RANK), slice_source, 0).reshape(
        tt_peers, cold_cap, E1 * RANK
    )
    terms = lax.all_to_all(grad_out, "tt", split_axis=0, concat_axis=0, tiled=True).reshape(
        -1, E1 * RANK
    )
    core_grad = owner_sum(wanted.reshape(-1), terms, slices_held, lax.Precision.DEFAULT)
    core_total = gathered_total(core_grad, "hot")
    new_first = core_first - 0.01 * core_total
    all_rows = jnp.concatenate([hot_rows, cold_rows], axis=0)
    all_picks = jnp.concatenate([hot_pick, cold_pick], axis=0)
    pooled = jnp.einsum("lb,le->be", all_picks, all_rows, preferred_element_type=jnp.float32)
    return (pooled, new_table, new_accum, new_first)


def solution(mesh):
    placed = (
        P("hot", None),
        P("hot"),
        P(("hot", "tt"), None),
        P(("hot", "tt"), None),
        P(("hot", "tt"), None),
        P(("hot", "tt"), None),
        P(("hot", "tt"), None),
        P(("hot", "tt"), None),
        P(("hot", "tt"), None),
        P(("hot", "tt"), None),
        P("tt", None),
        P(),
        P(),
        P(("hot", "tt"), None),
    )
    return jax.shard_map(
        local,
        mesh=mesh,
        in_specs=placed,
        out_specs=(P(("hot", "tt"), None), P("hot", None), P("hot"), P("tt", None)),
        check_vma=False,
    )
```

profile of v0, /device:TPU:1, one launch (start us, length us, event | category | flops | bytes accessed | tf_op | source)
XLA Modules:
  0.0 381.9 jit_solution(16041848748916325986)
XLA Ops:
  7.2 0.8 fusion.21
  8.0 1.1 reduce-window.16
  9.4 0.8 fusion.16
  10.8 2.4 scatter_custom_fusion.1
  13.3 6.2 %gather_fusion.5 = s32[1024]{0:T(1024)S(1)} fusion(s32[512]{0:T(512)} %bitcast.114, s32[1024]{0:T(1024)S(1)} %fusion.22), kind=kCustom, calls=%fused_computation.5 | custom fusion | bytes 12288 | tf_op jit(solution)/shard_map/jit(_take)/gather | solution.py:55
  20.2 15.7 %all-to-all-start.2 = ((s32[16,1,64]{2,1,0:T(1,128)}), s32[16,1,64]{2,1,0:T(1,128)S(1)}, u32[]{:S(2)}, u32[]{:S(2)}) async-start(s32[16,1,64]{2,1,0:T(1,128)} %select_n.97), calls=%async_computation.2 | async-start | bytes 16384 | tf_op jit(solution)/shard_map/all_to_all | solution.py:152
  35.9 144.4 %while.2 = (s32[]{:T(128)}, bf16[4,128,1024]{2,1,0:T(8,128)(2,1)}, s32[4,128]{1,0:T(4,128)}, bf16[64,8192]{1,0:T(8,128)(2,1)S(1)}, s32[4,128]{1,0:T(4,128)}, /*index=5*/bf16[64,128]{1,0:T(8,128)(2,1)S(1)}, s32[]{:T(128)}) while((s32[]{:T(128)}, bf16[4,128,1024]{2,1,0:T(8,128)(2,1)}, s32[4,128]{1,0:T(4,128)}, bf16[64,8192]{1,0:T(8,128)(2,1)S(1)}, ...), condition=%wide.region_9.10_spmd, body=%wide.region_8.9_spmd.sunk | while | flops 8522498 | bytes 16756829 | solution.py:88
  36.7 3.2 gather_fusion
  39.9 3.2 copy.76
  43.1 11.7 %copy.77 = bf16[128,32,8,32]{3,1,2,0:T(8,128)(2,1)} copy(bf16[128,32,8,32]{0,3,2,1:T(8,128)(2,1)S(1)} %bitcast.116) | data formatting | bytes 4194304 | tf_op jit(solution)/shard_map/while/body/eval_jaxpr/reshape | solution.py:81
  55.8 14.3 %convolution_convert_fusion.5 = bf16[128,32,8,4]{1,3,2,0:T(4,128)(2,1)S(1)} fusion(bf16[128,32,8,32]{3,1,2,0:T(8,128)(2,1)} %copy.77, bf16[128,32,4,1]{1,2,3,0:T(4,128)(2,1)S(1)} %copy.79), kind=kOutput, calls=%fused_computation.12.clone.1 | convolution fusion | flops 8519680 | bytes 2392064 | tf_op jit(solution)/shard_map/while/body/eval_jaxpr/nawb,nbe->nawe/dot_general | solution.py:83
  70.1 1.1 copy.80
  71.3 0.7 constant_dynamic-update-slice_fusion.2
  72.8 3.2 gather_fusion
  76.0 3.2 copy.76
  79.2 11.7 %copy.77 = bf16[128,32,8,32]{3,1,2,0:T(8,128)(2,1)} copy(bf16[128,32,8,32]{0,3,2,1:T(8,128)(2,1)S(1)} %bitcast.116) | data formatting | bytes 4194304 | tf_op jit(solution)/shard_map/while/body/eval_jaxpr/reshape | solution.py:81
  91.9 14.3 %convolution_convert_fusion.5 = bf16[128,32,8,4]{1,3,2,0:T(4,128)(2,1)S(1)} fusion(bf16[128,32,8,32]{3,1,2,0:T(8,128)(2,1)} %copy.77, bf16[128,32,4,1]{1,2,3,0:T(4,128)(2,1)S(1)} %copy.79), kind=kOutput, calls=%fused_computation.12.clone.1 | convolution fusion | flops 8519680 | bytes 2392064 | tf_op jit(solution)/shard_map/while/body/eval_jaxpr/nawb,nbe->nawe/dot_general | solution.py:83
  106.2 1.1 copy.80
  107.4 0.7 constant_dynamic-update-slice_fusion.2
  108.9 3.2 gather_fusion
  112.1 3.2 copy.76
  115.3 11.7 %copy.77 = bf16[128,32,8,32]{3,1,2,0:T(8,128)(2,1)} copy(bf16[128,32,8,32]{0,3,2,1:T(8,128)(2,1)S(1)} %bitcast.116) | data formatting | bytes 4194304 | tf_op jit(solution)/shard_map/while/body/eval_jaxpr/reshape | solution.py:81
  128.0 14.3 %convolution_convert_fusion.5 = bf16[128,32,8,4]{1,3,2,0:T(4,128)(2,1)S(1)} fusion(bf16[128,32,8,32]{3,1,2,0:T(8,128)(2,1)} %copy.77, bf16[128,32,4,1]{1,2,3,0:T(4,128)(2,1)S(1)} %copy.79), kind=kOutput, calls=%fused_computation.12.clone.1 | convolution fusion | flops 8519680 | bytes 2392064 | tf_op jit(solution)/shard_map/while/body/eval_jaxpr/nawb,nbe->nawe/dot_general | solution.py:83
  142.3 1.1 copy.80
  143.5 0.7 constant_dynamic-update-slice_fusion.2
  145.0 3.2 gather_fusion
  148.2 3.2 copy.76
  151.4 11.7 %copy.77 = bf16[128,32,8,32]{3,1,2,0:T(8,128)(2,1)} copy(bf16[128,32,8,32]{0,3,2,1:T(8,128)(2,1)S(1)} %bitcast.116) | data formatting | bytes 4194304 | tf_op jit(solution)/shard_map/while/body/eval_jaxpr/reshape | solution.py:81
  164.1 14.3 %convolution_convert_fusion.5 = bf16[128,32,8,4]{1,3,2,0:T(4,128)(2,1)S(1)} fusion(bf16[128,32,8,32]{3,1,2,0:T(8,128)(2,1)} %copy.77, bf16[128,32,4,1]{1,2,3,0:T(4,128)(2,1)S(1)} %copy.79), kind=kOutput, calls=%fused_computation.12.clone.1 | convolution fusion | flops 8519680 | bytes 2392064 | tf_op jit(solution)/shard_map/while/body/eval_jaxpr/nawb,nbe->nawe/dot_general | solution.py:83
  178.4 1.1 copy.80
  179.6 0.7 constant_dynamic-update-slice_fusion.2
  180.4 6.3 %reshape.380 = bf16[512,32,32]{2,1,0:T(8,128)(2,1)} reshape(bf16[4,128,1024]{2,1,0:T(8,128)(2,1)} %get-tuple-element.66) | data formatting | bytes 2097152 | tf_op jit(solution)/shard_map/reshape;reshape | solution.py:156
  187.0 0.8 copy.55
  187.8 4.4 %fusion.31 = bf16[512,8,32]{2,1,0:T(8,128)(2,1)S(1)} fusion(bf16[512,8,32]{2,1,0:T(8,128)(2,1)S(1)} %copy.55, bf16[512,32,32]{2,1,0:T(8,128)(2,1)} %reshape.380), kind=kOutput, calls=%fused_computation.93 | convolution fusion | flops 8388608 | bytes 1572864 | tf_op jit(solution)/shard_map/kej,kaj->kea/dot_general | solution.py:159
  192.2 0.7 copy.57
  193.1 4.1 %gather_fusion.9 = bf16[1024,256]{1,0:T(8,128)(2,1)S(1)} fusion(bf16[512,256]{1,0:T(8,128)(2,1)S(1)} %copy.58, s32[1024]{0:T(1024)S(1)} %fusion.22), kind=kCustom, calls=%fused_computation.9 | custom fusion | bytes 1052672 | tf_op jit(solution)/shard_map/jit(_take)/gather | solution.py:55
  197.3 1.0 broadcast_select_fusion
  198.3 11.6 %all-to-all-start.6 = ((bf16[16,64,256]{2,1,0:T(8,128)(2,1)}), bf16[16,64,256]{2,1,0:T(8,128)(2,1)S(1)}, u32[]{:S(2)}, u32[]{:S(2)}) async-start(bf16[16,64,256]{2,1,0:T(8,128)(2,1)} %broadcast_select_fusion), calls=%async_computation.6 | async-start | bytes 1048576 | tf_op jit(solution)/shard_map/all_to_all | solution.py:168
  211.3 21.7 %all-to-all-done.6 = bf16[16,64,256]{2,1,0:T(8,128)(2,1)S(1)} async-done(((bf16[16,64,256]{2,1,0:T(8,128)(2,1)}), bf16[16,64,256]{2,1,0:T(8,128)(2,1)S(1)}, u32[]{:S(2)}, u32[]{:S(2)}) %all-to-all-start.6) | async-done | bytes 524320 | tf_op jit(solution)/shard_map/all_to_all | solution.py:168
  233.0 0.9 fusion.4
  234.9 1.4 scatter_custom_fusion
  236.3 3.5 gather_fusion.2
  240.6 13.9 %all-to-all-start = ((s32[32,1,16]{2,1,0:T(1,128)}), s32[32,1,16]{2,1,0:T(1,128)S(1)}, u32[]{:S(2)}, u32[]{:S(2)}) async-start(s32[32,1,16]{2,1,0:T(1,128)} %bitcast.16), calls=%async_computation | async-start | bytes 32768 | tf_op jit(solution)/shard_map/all_to_all | solution.py:122
  254.7 2.0 gather_fusion.8
  256.8 0.9 broadcast_select_fusion.1
  257.6 3.7 all-to-all-done
  261.4 4.2 %all-to-all-start.4 = ((bf16[32,16,256]{2,1,0:T(8,128)(2,1)}), bf16[32,16,256]{2,1,0:T(8,128)(2,1)S(1)}, u32[]{:S(2)}, u32[]{:S(2)}) async-start(bf16[32,16,256]{2,1,0:T(8,128)(2,1)} %broadcast_select_fusion.1), calls=%async_computation.4 | async-start | bytes 524288 | tf_op jit(solution)/shard_map/all_to_all | solution.py:130
  265.6 0.7 fusion.29
  266.4 2.2 gather_fusion.3
  268.6 5.9 %all-to-all-done.4 = bf16[32,16,256]{2,1,0:T(8,128)(2,1)S(1)} async-done(((bf16[32,16,256]{2,1,0:T(8,128)(2,1)}), bf16[32,16,256]{2,1,0:T(8,128)(2,1)S(1)}, u32[]{:S(2)}, u32[]{:S(2)}) %all-to-all-start.4) | async-done | bytes 262176 | tf_op jit(solution)/shard_map/all_to_all | solution.py:130
  274.5 3.8 all-to-all-start.1
  278.4 1.0 fusion.5
  279.4 7.8 %all-to-all-done.1 = bf16[32,16,256]{2,1,0:T(8,128)(2,1)S(1)} async-done(((bf16[32,16,256]{2,1,0:T(8,128)(2,1)}), bf16[32,16,256]{2,1,0:T(8,128)(2,1)S(1)}, u32[]{:S(2)}, u32[]{:S(2)}) %all-to-all-start.1) | async-done | bytes 262176 | tf_op jit(solution)/shard_map/all_to_all | solution.py:124
  287.2 6.5 %all-to-all-start.5 = ((f32[16,16,256]{2,1,0:T(8,128)}), f32[16,16,256]{2,1,0:T(8,128)S(1)}, u32[]{:S(2)}, u32[]{:S(2)}) async-start(f32[16,16,256]{2,1,0:T(8,128)} %fusion.5), calls=%async_computation.5 | async-start | bytes 524288 | tf_op jit(solution)/shard_map/all_to_all | solution.py:22
  293.8 4.6 %gather_fusion.6 = bf16[1024,256]{1,0:T(8,128)(2,1)} fusion(f32[128,256]{1,0:T(8,128)S(1)} %copy-done.3, s32[1024]{0:T(1024)S(1)} %broadcast_clamp_fusion), kind=kCustom, calls=%fused_computation.6 | custom fusion | bytes 1052672 | tf_op jit(solution)/shard_map/gather | solution.py:153
  298.4 9.5 %all-to-all-done.5 = f32[16,16,256]{2,1,0:T(8,128)S(1)} async-done(((f32[16,16,256]{2,1,0:T(8,128)}), f32[16,16,256]{2,1,0:T(8,128)S(1)}, u32[]{:S(2)}, u32[]{:S(2)}) %all-to-all-start.5) | async-done | bytes 262176 | tf_op jit(solution)/shard_map/all_to_all | solution.py:22
  307.9 10.1 %all-to-all-start.3 = ((bf16[16,64,256]{2,1,0:T(8,128)(2,1)}), bf16[16,64,256]{2,1,0:T(8,128)(2,1)S(1)}, u32[]{:S(2)}, u32[]{:S(2)}) async-start(bf16[16,64,256]{2,1,0:T(8,128)(2,1)} %bitcast.25), calls=%async_computation.3 | async-start | bytes 1048576 | tf_op jit(solution)/shard_map/all_to_all | solution.py:154
  318.3 1.2 gather_fusion.4
  319.9 42.7 %all_gather.6 = f32[256,257]{1,0:T(8,128)S(1)} all-gather(f32[16,257]{1,0:T(8,128)S(1)} %pad_maximum_fusion), channel_id=1, replica_groups=mesh['hot'=32,'tt'=16] {'tt'}, dimensions={0}, use_global_device_ids=true | all-gather | bytes 279616 | tf_op jit(solution)/shard_map/all_gather | solution.py:31
  364.1 1.9 gather_fusion.7
  366.2 0.8 copy.50
  366.9 3.4 convolution_convert_fusion.1
  371.1 0.9 fusion.7
  372.0 2.4 reduce_sum.55
  (104 shorter events, 16.8 us)
Async XLA Ops:
  7.2 179.5 %copy-start = (bf16[64,256]{1,0:T(8,128)(2,1)S(1)}, bf16[64,256]{1,0:T(8,128)(2,1)}, u32[]{:S(2)}) copy-start(bf16[64,256]{1,0:T(8,128)(2,1)} %param.29) | copy-start | bytes 98308
  7.2 28.8 %copy-start.1 = (bf16[64,8192]{1,0:T(8,128)(2,1)S(1)}, bf16[64,8192]{1,0:T(8,128)(2,1)}, u32[]{:S(2)}) copy-start(bf16[64,8192]{1,0:T(8,128)(2,1)} %param.27) | copy-start | bytes 3145732
  7.2 28.8 %copy-start.4 = (bf16[64,128]{1,0:T(8,128)(2,1)S(1)}, bf16[64,128]{1,0:T(8,128)(2,1)}, u32[]{:S(2)}) copy-start(bf16[64,128]{1,0:T(8,128)(2,1)} %param.28) | copy-start | bytes 49156
  20.2 178.2 %all-to-all-start.2 = ((s32[16,1,64]{2,1,0:T(1,128)}), s32[16,1,64]{2,1,0:T(1,128)S(1)}, u32[]{:S(2)}, u32[]{:S(2)}) async-start(s32[16,1,64]{2,1,0:T(1,128)} %select_n.97), calls=%async_computation.2 | async-start | bytes 16384 | tf_op jit(solution)/shard_map/all_to_all | solution.py:152
  180.4 6.3 %copy-start.7 = (s32[1,512]{1,0:T(1,128)S(1)}, s32[1,512]{1,0:T(1,128)}, u32[]{:S(2)}) copy-start(s32[1,512]{1,0:T(1,128)} %param.25) | copy-start | bytes 6148
  193.0 41.0 %copy-start.6 = (s32[256,1]{0,1:T(1,128)S(1)}, s32[256,1]{0,1:T(1,128)}, u32[]{:S(2)}) copy-start(s32[256,1]{0,1:T(1,128)} %param.18) | copy-start | bytes 3076
  193.0 43.4 %copy-start.2 = (s32[1,256]{1,0:T(1,128)S(1)}, s32[1,256]{1,0:T(1,128)}, u32[]{:S(2)}) copy-start(s32[1,256]{1,0:T(1,128)} %param.19) | copy-start | bytes 3076
  193.1 61.4 %copy-start.8 = (s32[1,256]{1,0:T(1,128)S(1)}, s32[1,256]{1,0:T(1,128)}, u32[]{:S(2)}) copy-start(s32[1,256]{1,0:T(1,128)} %param.20) | copy-start | bytes 3076
  198.3 68.1 %copy-start.5 = (f32[256,256]{1,0:T(8,128)S(1)}, f32[256,256]{1,0:T(8,128)}, u32[]{:S(2)}) copy-start(f32[256,256]{1,0:T(8,128)} %param.16) | copy-start | bytes 786436
  198.3 34.7 %all-to-all-start.6 = ((bf16[16,64,256]{2,1,0:T(8,128)(2,1)}), bf16[16,64,256]{2,1,0:T(8,128)(2,1)S(1)}, u32[]{:S(2)}, u32[]{:S(2)}) async-start(bf16[16,64,256]{2,1,0:T(8,128)(2,1)} %broadcast_select_fusion), calls=%async_computation.6 | async-start | bytes 1048576 | tf_op jit(solution)/shard_map/all_to_all | solution.py:168
  209.9 162.0 %all-gather.3.cloned.1.call-start = ((), (), s32[]{:S(2)}) async-start(), calls=%async_computation.7 | async-start | bytes 4325376 | tf_op jit(solution)/shard_map/all_gather | solution.py:39
  239.9 53.9 %copy-start.3 = (f32[128,256]{1,0:T(8,128)S(1)}, f32[128,256]{1,0:T(8,128)}, u32[]{:S(2)}) copy-start(f32[128,256]{1,0:T(8,128)} %param.26) | copy-start | bytes 393220
  240.6 20.8 %all-to-all-start = ((s32[32,1,16]{2,1,0:T(1,128)}), s32[32,1,16]{2,1,0:T(1,128)S(1)}, u32[]{:S(2)}, u32[]{:S(2)}) async-start(s32[32,1,16]{2,1,0:T(1,128)} %bitcast.16), calls=%async_computation | async-start | bytes 32768 | tf_op jit(solution)/shard_map/all_to_all | solution.py:122
  261.4 13.2 %all-to-all-start.4 = ((bf16[32,16,256]{2,1,0:T(8,128)(2,1)}), bf16[32,16,256]{2,1,0:T(8,128)(2,1)S(1)}, u32[]{:S(2)}, u32[]{:S(2)}) async-start(bf16[32,16,256]{2,1,0:T(8,128)(2,1)} %broadcast_select_fusion.1), calls=%async_computation.4 | async-start | bytes 524288 | tf_op jit(solution)/shard_map/all_to_all | solution.py:130
  274.5 12.7 %all-to-all-start.1 = ((bf16[32,16,256]{2,1,0:T(8,128)(2,1)}), bf16[32,16,256]{2,1,0:T(8,128)(2,1)S(1)}, u32[]{:S(2)}, u32[]{:S(2)}) async-start(bf16[32,16,256]{2,1,0:T(8,128)(2,1)} %bitcast.17), calls=%async_computation.1 | async-start | bytes 524288 | tf_op jit(solution)/shard_map/all_to_all | solution.py:124
  279.4 40.2 %copy-start.9 = (f32[256]{0:T(256)S(1)}, f32[256]{0:T(256)}, u32[]{:S(2)}) copy-start(f32[256]{0:T(256)} %param.17) | copy-start | bytes 3076
  287.2 20.7 %all-to-all-start.5 = ((f32[16,16,256]{2,1,0:T(8,128)}), f32[16,16,256]{2,1,0:T(8,128)S(1)}, u32[]{:S(2)}, u32[]{:S(2)}) async-start(f32[16,16,256]{2,1,0:T(8,128)} %fusion.5), calls=%async_computation.5 | async-start | bytes 524288 | tf_op jit(solution)/shard_map/all_to_all | solution.py:22
  307.9 56.2 %all-to-all-start.3 = ((bf16[16,64,256]{2,1,0:T(8,128)(2,1)}), bf16[16,64,256]{2,1,0:T(8,128)(2,1)S(1)}, u32[]{:S(2)}, u32[]{:S(2)}) async-start(bf16[16,64,256]{2,1,0:T(8,128)(2,1)} %bitcast.25), calls=%async_computation.3 | async-start | bytes 1048576 | tf_op jit(solution)/shard_map/all_to_all | solution.py:154
Sparse Core Ops, SparseCore 0:
  234.1 64.4 all-gather.2
where the time goes:
time: 388 us; the launch traced here: 382 us
  local copies, waits for them, and re-layouts  128 us (33%)
  matrix products  68.2 us (18%)
  starting transfers between devices  65.8 us (17%)
  waiting for transfers between devices  48.8 us (13%)
  blocking collectives  42.7 us (11%)
  between operations  14.5 us (4%)
  other arithmetic  14 us (4%)
    dot_general x4, matrix products, rank_one_block(): jnp.einsum('nawb,nbe->nawe', mid_cores, last_cores, preferred_element_typ...  57 us
    reshape x4, local copies, waits for them, and re-layouts, rank_one_block(): mid_cores = core_mid[mid_part].reshape(-1, RANK, E2, RANK)  46.9 us
    all_gather x1, blocking collectives, in_one_piece(): result = lax.all_gather(both, axis, axis=dim, tiled=True)  42.7 us
    gather x8, local copies, waits for them, and re-layouts, rank_one_block(): mid_cores = core_mid[mid_part].reshape(-1, RANK, E2, RANK)  25.7 us
    all_to_all x1, waiting for transfers between devices, local(): lax.all_to_all(grad_out, 'tt', split_axis=0, concat_axis=0, tiled=True)  21.7 us
    gather x4, local copies, waits for them, and re-layouts, packed(): return jnp.take(values, source, axis=0, mode='fill', fill_value=fill_value)  15.8 us
    all_to_all x1, starting transfers between devices, local(): lax.all_to_all(slice_request, 'tt', split_axis=0, concat_axis=0, tiled=True)  15.7 us
    all_to_all x1, starting transfers between devices, local(): lax.all_to_all(request, 'hot', split_axis=0, concat_axis=0, tiled=True)  13.9 us
  transfers between devices with their start and end apart: 8, of which 5 were waited for; matrix products, arithmetic and copies ran while one was open for 51% of the time, Pallas kernels for 0%

commit v1 on v0

v1 whole, which is shorter than its diff:
```python
import functools

import jax
import jax.numpy as jnp
from jax import lax
from jax.experimental import pallas as pl
from jax.experimental.pallas import tpu as pltpu
from jax.sharding import PartitionSpec as P

MESH = pl.DeviceIdType.MESH
F32 = jnp.float32
BF16 = jnp.bfloat16

HOTS = 32
TTS = 16
CHIPS = 16
E1, E2, E3, RANK = 8, 8, 4, 32
CAP = 16
HL = 256
CL = 512
BAGS = 64
E = 256
ROWS = 256
SL = 128
MIDS = 64


def nn(a, b):
    return jnp.dot(a, b, preferred_element_type=F32)


def tn(a, b):
    return lax.dot_general(a, b, (((0,), (0,)), ((), ())), preferred_element_type=F32)


def nt(a, b):
    return lax.dot_general(a, b, (((1,), (1,)), ((), ())), preferred_element_type=F32)


def iota(shape, dim):
    return lax.broadcasted_iota(jnp.int32, shape, dim)


def send(src, dst, ssem, rsem, hot, tt):
    pltpu.make_async_remote_copy(
        src_ref=src,
        dst_ref=dst,
        send_sem=ssem,
        recv_sem=rsem,
        device_id=(hot, tt),
        device_id_type=MESH,
    ).start()


def wait(ref, sem):
    pltpu.make_async_copy(ref, ref, sem).wait()


def kernel(
    ht, ha, ho, hr, hb, co, fi, mi, li, cb, cf, mid, last, bg,
    pooled, ntab, nacc, nfirst,
    ids_s, ids_r, hs, hrv, rs, rr, zs, zr, gs, gr,
    G, T, LHS, RHS, M2, OHS, LT, cotT, slT, termsT, rowsT, SBs, RTs, pown, dsn, dr, qs, qr, czs, czr, fs, fr,
    ssem, rsem, c1z_sem, c2z_sem, fr_sem,
):
    h = lax.axis_index("hot")
    t = lax.axis_index("tt")
    c = h // 2
    k = lax.rem(h, 2)
    rg = c // 2
    ch = lax.rem(c, 2)
    tp_me = t // 2
    mine = lax.rem(t, 2) == k

    def rows16(r):
        return pl.ds(pl.multiple_of(r * 16, 16), 16)

    def each(n, me, f):
        def step(d, _):
            f(lax.rem(me + d, n))
            return 0

        lax.fori_loop(1, n, step, 0)

    barrier = pltpu.get_barrier_semaphore()
    each(HOTS, h, lambda p: pl.semaphore_signal(barrier, inc=1, device_id=(p, t), device_id_type=MESH))
    each(TTS, t, lambda p: pl.semaphore_signal(barrier, inc=1, device_id=(h, p), device_id_type=MESH))

    ho_col = ho[...]
    oh_owner = (ho_col == iota((HL, HOTS), 1)).astype(F32)
    tri = (iota((HL, HL), 0) > iota((HL, HL), 1)).astype(BF16)
    eye = iota((HL, HL), 0) == iota((HL, HL), 1)
    before = nn(tri, oh_owner.astype(BF16))
    slot = jnp.sum(before * oh_owner, axis=1, keepdims=True).astype(jnp.int32)
    slot_pick = (ho_col * CAP + slot == iota((HL, HOTS * CAP), 1)).astype(BF16)
    hot_pick = (iota((BAGS, HL), 0) == hb[...]).astype(BF16)
    SBs[...] = nn(hot_pick, slot_pick).astype(BF16)
    hs[...] = tn(SBs[...], bg[...]).astype(BF16).reshape(HOTS, CAP, E)
    row_col = jnp.sum(jnp.where(eye, hr[...].astype(F32), 0.0), axis=1, keepdims=True)
    row_at = jnp.where(slot == iota((HL, 128), 1), row_col + 1.0, 0.0).astype(BF16)
    ids_s[...] = (tn(oh_owner.astype(BF16), row_at) - 1.0).reshape(HOTS, 1, 128)

    @pl.when(mine)
    def _():
        left = cf[rows16(rg), 0:128]
        right = cf[rows16(rg), 128:256]
        G[k, ch, tp_me, rows16(rg), :] = jnp.where(ch == 0, left, right).astype(BF16)

    pl.semaphore_wait(barrier, HOTS - 1 + TTS - 1)

    each(HOTS, h, lambda p: send(ids_s.at[p], ids_r.at[h], ssem.at[0], rsem.at[0], p, t))

    @pl.when(mine)
    def _():
        piece = G.at[k, ch, tp_me, rows16(rg), :]
        each(TTS, t, lambda p: send(piece, piece, ssem.at[1], c1z_sem.at[tp_me], h, p))

    each(HOTS, h, lambda p: send(hs.at[p], hrv.at[h], ssem.at[2], rsem.at[2], p, t))
    ids_r[h] = ids_s[h]
    hrv[h] = hs[h]

    eye_c = iota((CL, CL), 0) == iota((CL, CL), 1)
    owner = jnp.sum(jnp.where(eye_c, co[...].astype(F32), 0.0), axis=0, keepdims=True).astype(jnp.int32)
    key = (owner & 1) * 1024 + (owner >> 1) * SL + fi[...]
    for n in range(4):
        OHS[n * 512 : (n + 1) * 512, :] = (iota((512, CL), 0) + n * 512 == key).astype(BF16)
    cold_pick = (iota((BAGS, CL), 0) == cb[...]).astype(BF16)
    cot = tn(bg[...], cold_pick)
    for n in range(4):
        rowsT[n] = cot[:, n * 128 : (n + 1) * 128]
        for e in range(E3):
            cotT[n, e] = rowsT[n, pl.ds(e, 64, stride=E3), :]
    last_pick = (iota((MIDS, CL), 0) == li[...]).astype(BF16)
    picked = tn(last[...], last_pick)
    for n in range(4):
        M2[n, 0:128, :] = picked[:, n * 128 : (n + 1) * 128]
        for e in range(E3):
            LT[e, :, n * 128 : (n + 1) * 128] = M2[n, pl.ds(e, RANK, stride=E3), :]

    def turn(j, _):
        blk = mid[:, pl.ds(pl.multiple_of(j * 128, 128), 128)].astype(F32).T
        parts = blk.reshape(4, 2, 16, MIDS)
        wide = jnp.concatenate([parts[:, 0], parts[:, 1]], axis=-1).reshape(64, 128)
        T[pl.ds(pl.multiple_of(j * 64, 64), 64), :] = wide
        return 0

    lax.fori_loop(0, 64, turn, 0)
    for n in range(16):
        LHS[:, n * 128 : (n + 1) * 128] = T[pl.ds(n, 256, stride=16), :].astype(BF16)

    wait(ids_r.at[pl.ds(0, HOTS - 1)], rsem.at[0])
    asked = jnp.broadcast_to(ids_r[...], (HOTS, CAP, 128)).reshape(HOTS * CAP, 128)
    at_slot = iota((HOTS * CAP, 128), 1) == lax.rem(iota((HOTS * CAP, 128), 0), CAP)
    asked = jnp.sum(jnp.where(at_slot, asked, 0.0), axis=1, keepdims=True).astype(jnp.int32)
    RTs[...] = (asked == iota((HOTS * CAP, ROWS), 1)).astype(BF16)
    rs[...] = nn(RTs[...], ht[...].astype(BF16)).astype(BF16).reshape(HOTS, CAP, E)
    each(HOTS, h, lambda p: send(rs.at[p], rr.at[h], ssem.at[3], rsem.at[3], p, t))
    rr[h] = rs[h]

    wait(hrv.at[pl.ds(0, HOTS - 1)], rsem.at[2])
    zs[...] = tn(RTs[...], hrv[...].reshape(HOTS * CAP, E)).astype(BF16).reshape(TTS, CAP, E)
    each(TTS, t, lambda p: send(zs.at[p], zr.at[t], ssem.at[4], rsem.at[4], h, p))
    zr[t] = zs[t]

    def from_plane(tp, _):
        @pl.when(tp * 2 + k != t)
        def _():
            wait(G.at[k, ch, 0, rows16(rg), :], c1z_sem.at[tp])

        return 0

    lax.fori_loop(0, 8, from_plane, 0)
    piece8 = G.at[k, ch, :, rows16(rg), :]
    each(CHIPS, c, lambda p: send(piece8, piece8, ssem.at[5], rsem.at[5], p * 2 + k, t))

    def one_e(e, _):
        is_mid = iota((MIDS, CL), 0) == mi[...]
        for n in range(32):
            b = (n % 2) * 16 + n // 2
            row = LT[e, b : b + 1, :]
            RHS[n * MIDS : (n + 1) * MIDS, :] = jnp.where(is_mid, row, 0.0).astype(BF16)
        made = nn(LHS[...], RHS[...])
        made = made.astype(BF16).astype(F32)
        for n in range(4):
            M2[n, pl.ds(pl.multiple_of(e * 256, 256), 256), :] = made[:, n * 128 : (n + 1) * 128]
        return 0

    lax.fori_loop(0, E3, one_e, 0)

    wait(zr.at[pl.ds(0, TTS - 1)], rsem.at[4])
    gs[...] = jnp.sum(zr[...].astype(F32), axis=0).astype(BF16)
    each(TTS, t, lambda p: send(gs, gr.at[t], ssem.at[6], rsem.at[6], h, p))
    gr[t] = gs[...]

    wait(qr.at[pl.ds(0, CHIPS - 1)], rsem.at[5])
    send(G.at[k], G.at[k], ssem.at[7], rsem.at[7], c * 2 + 1 - k, t)

    def back_lanes(kt, _):
        def back_e(e, acc):
            acc = list(acc)
            for w in range(E2):
                tiles = [M2[kt, pl.ds(e * 256 + ab * 64 + w, 8, stride=8), :] for ab in range(4)]
                for e1 in range(E1):
                    cot = cotT[kt, e, e1 * 8 + w : e1 * 8 + w + 1, :]
                    for ab in range(4):
                        acc[e1 * 4 + ab] = acc[e1 * 4 + ab] + cot * tiles[ab]
            return tuple(acc)

        acc = lax.fori_loop(0, E3, back_e, tuple(jnp.zeros((8, 128), F32) for _ in range(32)))
        for i in range(32):
            termsT[kt, i * 8 : (i + 1) * 8, :] = acc[i]
        return 0

    lax.fori_loop(0, 4, back_lanes, 0)
    terms = jnp.concatenate([termsT[n] for n in range(4)], axis=1).astype(BF16)

    def half(which):
        return OHS[pl.ds(pl.multiple_of(which * 1024, 1024), 1024), :]

    other = nt(half(1 - k), terms).astype(BF16)
    dsn[0] = other[:, :128].reshape(8, SL, 128)
    dsn[1] = other[:, 128:].reshape(8, SL, 128)
    send(dsn, dr, ssem.at[8], rsem.at[8], c * 2 + 1 - k, t)
    pown[...] = nt(half(k), terms)

    wait(dr, rsem.at[8])
    for i in range(2):
        mine_f = pown[:, i * 128 : (i + 1) * 128].reshape(8, SL, 128)
        qs[i] = (mine_f + dr[i].astype(F32)).astype(BF16)

    def to_chip(p):
        src = qs.at[lax.rem(p, 2), :, rows16(p // 2), :]
        send(src, qr.at[c], ssem.at[9], rsem.at[9], p * 2 + k, t)

    each(CHIPS, c, to_chip)
    qr[c] = qs[ch, :, rows16(rg), :]

    wait(G.at[0], rsem.at[7])
    for i in range(2):
        got = tn(G[0, i].reshape(1024, 128), OHS[0:1024, :]) + tn(G[1, i].reshape(1024, 128), OHS[1024:2048, :])
        for j in range(16):
            for n in range(4):
                at = (i * 4 + j // 4) * 8
                slT[n, j % 4, at : at + 8, :] = got[j * 8 : (j + 1) * 8, n * 128 : (n + 1) * 128]

    def fore_lanes(kt, _):
        def fore_a(a8, acc):
            acc = list(acc)
            for ai in range(8):
                a = a8 * 8 + ai
                tiles = [M2[kt, pl.ds(pl.multiple_of(e * 256 + a * 8, 8), 8), :] for e in range(E3)]
                for e1 in range(E1):
                    row = slT[kt, a8, e1 * 8 + ai : e1 * 8 + ai + 1, :]
                    for e in range(E3):
                        acc[e1 * 4 + e] = acc[e1 * 4 + e] + row * tiles[e]
            return tuple(acc)

        acc = lax.fori_loop(0, 4, fore_a, tuple(jnp.zeros((8, 128), F32) for _ in range(32)))
        for e1 in range(E1):
            for e in range(E3):
                rowsT[kt, pl.ds(e1 * 32 + e, 8, stride=E3), :] = acc[e1 * 4 + e]
        return 0

    lax.fori_loop(0, 4, fore_lanes, 0)
    cold_pick = (iota((BAGS, CL), 0) == cb[...]).astype(BF16)
    rows_bf = jnp.concatenate([rowsT[n] for n in range(4)], axis=1).astype(BF16)
    wait(rr.at[pl.ds(0, HOTS - 1)], rsem.at[3])
    pooled[...] = nt(cold_pick, rows_bf) + nn(SBs[...], rr[...].reshape(HOTS * CAP, E))

    wait(qr.at[pl.ds(0, CHIPS - 1)], rsem.at[9])
    total = qr[0].astype(F32)
    for i in range(1, CHIPS):
        total = total + qr[i].astype(F32)
    czs[...] = total.astype(BF16)

    def to_owner(tp, _):
        @pl.when(tp * 2 + k != t)
        def _():
            send(czs.at[tp], czr.at[t], ssem.at[10], c2z_sem.at[t], h, tp * 2 + k)

        return 0

    lax.fori_loop(0, 8, to_owner, 0)

    wait(gr.at[pl.ds(0, TTS - 1)], rsem.at[6])
    grad = gr[...].reshape(ROWS, E).astype(F32)
    accum = jnp.sum(jnp.where(eye, ha[...], 0.0), axis=1, keepdims=True)
    accum = accum + jnp.sum(grad * grad, axis=1, keepdims=True) * (1.0 / E)
    ntab[...] = ht[...] - 0.1 * grad / (jnp.sqrt(accum) + 1e-08)
    nacc[...] = jnp.sum(jnp.where(eye, accum, 0.0), axis=0, keepdims=True)

    @pl.when(mine)
    def _():
        czr[t] = czs[tp_me]

        def from_tt(p, _):
            @pl.when(p != t)
            def _():
                wait(czr.at[0], c2z_sem.at[p])

            return 0

        lax.fori_loop(0, TTS, from_tt, 0)
        fs[...] = jnp.sum(czr[...].astype(F32), axis=0)
        fr[c] = fs[...]
        each(HOTS, h, lambda p: send(fs, fr.at[c], ssem.at[11], fr_sem.at[c], p, t))

    def from_chip(p, _):
        @pl.when(p * 2 + lax.rem(t, 2) != h)
        def _():
            wait(fr.at[0], fr_sem.at[p])

        return 0

    lax.fori_loop(0, CHIPS, from_chip, 0)
    for p in range(CHIPS):
        at = (slice((p // 2) * 16, (p // 2) * 16 + 16), slice((p % 2) * 128, (p % 2) * 128 + 128))
        nfirst[at] = cf[at] - 0.01 * fr[p]

    wait(ids_r.at[pl.ds(0, HOTS - 1)], ssem.at[0])
    wait(hrv.at[pl.ds(0, HOTS - 1)], ssem.at[2])
    wait(rr.at[pl.ds(0, HOTS - 1)], ssem.at[3])
    wait(zr.at[pl.ds(0, TTS - 1)], ssem.at[4])
    wait(qr.at[pl.ds(0, CHIPS - 1)], ssem.at[5])
    wait(gr.at[pl.ds(0, TTS - 1)], ssem.at[6])
    wait(G.at[0], ssem.at[7])
    wait(dsn, ssem.at[8])
    wait(qr.at[pl.ds(0, CHIPS - 1)], ssem.at[9])

    @pl.when(mine)
    def _():
        wait(czr.at[pl.ds(0, TTS - 1)], ssem.at[1])
        wait(czr.at[pl.ds(0, 7)], ssem.at[10])
        wait(fr.at[pl.ds(0, HOTS - 1)], ssem.at[11])

    @pl.when(jnp.logical_not(mine))
    def _():
        wait(czr.at[pl.ds(0, 8)], ssem.at[10])


def local(
    hot_table, hot_accum, hot_owner, hot_row, hot_bag, cold_owner, first_index, mid_index, last_index, cold_bag,
    core_first, core_mid, core_last, bag_grads,
):
    vm = pl.BlockSpec(memory_space=pltpu.VMEM)
    v = pltpu.VMEM
    outs = (
        jax.ShapeDtypeStruct((BAGS, E), F32),
        jax.ShapeDtypeStruct((ROWS, E), F32),
        jax.ShapeDtypeStruct((1, ROWS), F32),
        jax.ShapeDtypeStruct((SL, E), F32),
    )
    scratch = [
        v((HOTS, 1, 128), F32),
        v((HOTS, 1, 128), F32),
        v((HOTS, CAP, E), BF16),
        v((HOTS, CAP, E), BF16),
        v((HOTS, CAP, E), BF16),
        v((HOTS, CAP, E), BF16),
        v((TTS, CAP, E), BF16),
        v((TTS, CAP, E), BF16),
        v((CAP, E), BF16),
        v((TTS, CAP, E), BF16),
        v((2, 2, 8, SL, 128), BF16),
        v((4096, 128), F32),
        v((256, 2048), BF16),
        v((2048, CL), BF16),
        v((4, 1024, 128), F32),
        v((2048, CL), BF16),
        v((E3, RANK, CL), F32),
        v((4, E3, 64, 128), F32),
        v((4, 4, 64, 128), F32),
        v((4, E, 128), F32),
        v((4, E, 128), F32),
        v((BAGS, HOTS * CAP), BF16),
        v((HOTS * CAP, ROWS), BF16),
        v((1024, E), F32),
        v((2, 8, SL, 128), BF16),
        v((2, 8, SL, 128), BF16),
        v((2, 8, SL, 128), BF16),
        v((CHIPS, 8, 16, 128), BF16),
        v((8, 16, 128), BF16),
        v((TTS, 16, 128), BF16),
        v((16, 128), F32),
        v((HOTS, 16, 128), F32),
        pltpu.SemaphoreType.DMA((12,)),
        pltpu.SemaphoreType.DMA((12,)),
        pltpu.SemaphoreType.DMA((8,)),
        pltpu.SemaphoreType.DMA((TTS,)),
        pltpu.SemaphoreType.DMA((CHIPS,)),
    ]
    pooled, new_table, new_accum, new_first = pl.pallas_call(
        kernel,
        out_shape=outs,
        in_specs=[vm] * 14,
        out_specs=(vm,) * 4,
        scratch_shapes=scratch,
        compiler_params=pltpu.CompilerParams(collective_id=0, has_side_effects=True),
    )(
        hot_table, hot_accum.reshape(1, ROWS), hot_owner, hot_row, hot_bag, cold_owner, first_index, mid_index,
        last_index, cold_bag, core_first, core_mid, core_last, bag_grads,
    )
    return pooled, new_table, new_accum.reshape(ROWS), new_first


def solution(mesh):
    both = P(("hot", "tt"), None)
    placed = (P("hot", None), P("hot"), *((both,) * 8), P("tt", None), P(), P(), both)
    return jax.shard_map(
        local,
        mesh=mesh,
        in_specs=placed,
        out_specs=(both, P("hot", None), P("hot"), P("tt", None)),
        check_vma=False,
    )
```

time: 388 us -> 78.6 us (0.20); the launches traced: 382 us -> 78.4 us
  local copies, waits for them, and re-layouts: 128 us -> 6.74 us
  Pallas kernels: 0 us -> 71 us
  matrix products: 68.2 us -> 0 us
  starting transfers between devices: 65.8 us -> 0 us
  waiting for transfers between devices: 48.8 us -> 0 us
  blocking collectives: 42.7 us -> 0 us
  other arithmetic: 14 us -> 0 us
  between operations: 14.5 us -> 0.65 us
    pallas_call x0 -> x1, Pallas kernels: none -> 71 us  [local(): pl.pallas_call(kernel, out_shape=outs, in_specs=[vm] * 14, out_specs=(vm,...]
    dot_general x11 -> x0, matrix products: 68.2 us -> none  [the longest x4 57 us: rank_one_block(): jnp.einsum('nawb,nbe->nawe', mid_cores, last_cores, preferred_element_typ...]
    all_to_all x7 -> x0, starting transfers between devices: 65.7 us -> none  [the longest x1 15.7 us: local(): lax.all_to_all(slice_request, 'tt', split_axis=0, concat_axis=0, tiled=True)]
    gather x26 -> x0, local copies, waits for them, and re-layouts: 54.9 us -> none  [the longest x8 25.7 us: rank_one_block(): mid_cores = core_mid[mid_part].reshape(-1, RANK, E2, RANK)]
    reshape x12 -> x0, local copies, waits for them, and re-layouts: 49.3 us -> none  [the longest x4 46.9 us: rank_one_block(): mid_cores = core_mid[mid_part].reshape(-1, RANK, E2, RANK)]
    all_to_all x7 -> x0, waiting for transfers between devices: 48.7 us -> none  [the longest x1 21.7 us: local(): lax.all_to_all(grad_out, 'tt', split_axis=0, concat_axis=0, tiled=True)]
    all_gather x1 -> x0, blocking collectives: 42.7 us -> none  [in_one_piece(): result = lax.all_gather(both, axis, axis=dim, tiled=True)]
    unnamed x20 -> x14, local copies, waits for them, and re-layouts: 0.05 us -> 6.74 us
  transfers between devices with their start and end apart: 8 -> 0, of which waited for: 5 -> 0; matrix products, arithmetic and copies ran while one was open for 51% -> 0% of each run, Pallas kernels for 0% -> 0%
where the time goes in v1:
time: 78.6 us; the launch traced here: 78.4 us
  Pallas kernels  71 us (90%)
  local copies, waits for them, and re-layouts  6.74 us (9%)
    pallas_call x1, Pallas kernels, local(): pl.pallas_call(kernel, out_shape=outs, in_specs=[vm] * 14, out_specs=(vm,...  71 us
    unnamed x14, local copies, waits for them, and re-layouts  6.74 us

profile of v1, /device:TPU:1, one launch (start us, length us, event | category | flops | bytes accessed | tf_op | source)
XLA Modules:
  0.0 78.4 jit_solution(1071474497769197473)
XLA Ops:
  0.6 0.0 copy-start.2
  0.6 0.7 copy-done.2
  1.3 0.0 copy-start.1
  1.3 0.8 %copy.18.ho = s32[256,1]{1,0:T(8,128)} copy(s32[256,1]{0,1:T(1,128)S(1)} %copy-done.2) | data formatting | bytes 2048 | tf_op args[2]
  2.1 0.0 copy-done.1
  2.1 0.9 %copy.19.co = s32[512,1]{1,0:T(8,128)} copy(s32[512,1]{0,1:T(1,128)S(1)} %copy-done.1) | data formatting | bytes 4096 | tf_op args[5]
  3.0 71.0 %shard_map.165 = (f32[64,256]{1,0:T(8,128)}, f32[256,256]{1,0:T(8,128)}, f32[1,256]{1,0:T(1,128)}, f32[128,256]{1,0:T(8,128)}) custom-call(f32[256,256]{1,0:T(8,128)} %ht.1, f32[1,256]{1,0:T(1,128)} %bitcast.2, s32[256,1]{1,0:T(8,128)} %copy.18.ho, s32[1,256]{1,0:T(1,128)} %hr.1, s32[1,256]{1,0:T(1,128)} %hb.1, s32[512,1]{1,0:T(8,128)} %copy.19.co, ...), custom_call_target="tpu_custom_call" | custom-call | tf_op jit(solution)/shard_map/pallas_call | solution.py:392
  74.0 1.5 %copy.24 = f32[64,256]{1,0:T(8,128)} copy(f32[64,256]{1,0:T(8,128)} %get-tuple-element.16) | data formatting | bytes 131072
  75.5 0.0 copy-start.3
  75.5 0.0 copy-start
  75.5 1.7 %copy.25 = f32[256,256]{1,0:T(8,128)} copy(f32[256,256]{1,0:T(8,128)} %get-tuple-element.17) | data formatting | bytes 524288
  77.2 0.0 copy-done.3
  77.2 0.6 copy.26
  77.7 0.0 copy-done
  77.7 0.7 copy.27
Async XLA Ops:
  0.6 0.7 copy-start.2
  1.3 0.8 %copy-start.1 = (s32[512,1]{0,1:T(1,128)S(1)}, s32[512,1]{0,1:T(1,128)}, u32[]{:S(2)}) copy-start(s32[512,1]{0,1:T(1,128)} %param.19) | copy-start | bytes 6148
  75.5 1.7 %copy-start.3 = (f32[1,256]{1,0:T(1,128)S(1)}, f32[1,256]{1,0:T(1,128)}, u32[]{:S(2)}) copy-start(f32[1,256]{1,0:T(1,128)} %get-tuple-element.10) | copy-start | bytes 3076
  75.5 2.3 %copy-start = (f32[128,256]{1,0:T(8,128)S(1)}, f32[128,256]{1,0:T(8,128)}, u32[]{:S(2)}) copy-start(f32[128,256]{1,0:T(8,128)} %get-tuple-element.19) | copy-start | bytes 393220

commit v2 on v1

--- a/solution.py
+++ b/solution.py
@@ -23,6 +23,7 @@
 ROWS = 256
 SL = 128
 MIDS = 64
+LIMIT = 36 * 1024 * 1024
 
 
 def nn(a, b):
@@ -57,12 +58,26 @@
 
 
 def kernel(
-    ht, ha, ho, hr, hb, co, fi, mi, li, cb, cf, mid, last, bg,
+    ho_h, hr_h, hb_h, bg_h, co_h, fi_h, cb_h, mi_h, li_h, last_h, cf_h, mid_h, ht_h, ha_h,
     pooled, ntab, nacc, nfirst,
+    ho, hr, hb, bg, co, fi, cb, mi, li, last, cf, mid, ht, ha,
     ids_s, ids_r, hs, hrv, rs, rr, zs, zr, gs, gr,
     G, T, LHS, RHS, M2, OHS, LT, cotT, slT, termsT, rowsT, SBs, RTs, pown, dsn, dr, qs, qr, czs, czr, fs, fr,
-    ssem, rsem, c1z_sem, c2z_sem, fr_sem,
+    isem, ssem, rsem, c1z_sem, c2z_sem, fr_sem,
 ):
+    ins = (ho_h, hr_h, hb_h, bg_h, co_h, fi_h, cb_h, mi_h, li_h, last_h, cf_h, mid_h, ht_h, ha_h)
+    held = (ho, hr, hb, bg, co, fi, cb, mi, li, last, cf, mid, ht, ha)
+
+    def fetch(i):
+        return pltpu.make_async_copy(ins[i], held[i], isem.at[i])
+
+    def need(*which):
+        for i in which:
+            fetch(i).wait()
+
+    for i in range(len(ins)):
+        fetch(i).start()
+
     h = lax.axis_index("hot")
     t = lax.axis_index("tt")
     c = h // 2
@@ -86,10 +101,11 @@
     each(HOTS, h, lambda p: pl.semaphore_signal(barrier, inc=1, device_id=(p, t), device_id_type=MESH))
     each(TTS, t, lambda p: pl.semaphore_signal(barrier, inc=1, device_id=(h, p), device_id_type=MESH))
 
-    ho_col = ho[...]
+    need(0, 1, 2, 3)
+    eye = iota((HL, HL), 0) == iota((HL, HL), 1)
+    ho_col = jnp.sum(jnp.where(eye, ho[...].astype(F32), 0.0), axis=1, keepdims=True).astype(jnp.int32)
     oh_owner = (ho_col == iota((HL, HOTS), 1)).astype(F32)
     tri = (iota((HL, HL), 0) > iota((HL, HL), 1)).astype(BF16)
-    eye = iota((HL, HL), 0) == iota((HL, HL), 1)
     before = nn(tri, oh_owner.astype(BF16))
     slot = jnp.sum(before * oh_owner, axis=1, keepdims=True).astype(jnp.int32)
     slot_pick = (ho_col * CAP + slot == iota((HL, HOTS * CAP), 1)).astype(BF16)
@@ -100,6 +116,7 @@
     row_at = jnp.where(slot == iota((HL, 128), 1), row_col + 1.0, 0.0).astype(BF16)
     ids_s[...] = (tn(oh_owner.astype(BF16), row_at) - 1.0).reshape(HOTS, 1, 128)
 
+    need(10)
     @pl.when(mine)
     def _():
         left = cf[rows16(rg), 0:128]
@@ -119,8 +136,8 @@
     ids_r[h] = ids_s[h]
     hrv[h] = hs[h]
 
-    eye_c = iota((CL, CL), 0) == iota((CL, CL), 1)
-    owner = jnp.sum(jnp.where(eye_c, co[...].astype(F32), 0.0), axis=0, keepdims=True).astype(jnp.int32)
+    need(4, 5, 6, 7, 8, 9)
+    owner = co[...]
     key = (owner & 1) * 1024 + (owner >> 1) * SL + fi[...]
     for n in range(4):
         OHS[n * 512 : (n + 1) * 512, :] = (iota((512, CL), 0) + n * 512 == key).astype(BF16)
@@ -137,6 +154,7 @@
         for e in range(E3):
             LT[e, :, n * 128 : (n + 1) * 128] = M2[n, pl.ds(e, RANK, stride=E3), :]
 
+    need(11)
     def turn(j, _):
         blk = mid[:, pl.ds(pl.multiple_of(j * 128, 128), 128)].astype(F32).T
         parts = blk.reshape(4, 2, 16, MIDS)
@@ -147,31 +165,6 @@
     lax.fori_loop(0, 64, turn, 0)
     for n in range(16):
         LHS[:, n * 128 : (n + 1) * 128] = T[pl.ds(n, 256, stride=16), :].astype(BF16)
-
-    wait(ids_r.at[pl.ds(0, HOTS - 1)], rsem.at[0])
-    asked = jnp.broadcast_to(ids_r[...], (HOTS, CAP, 128)).reshape(HOTS * CAP, 128)
-    at_slot = iota((HOTS * CAP, 128), 1) == lax.rem(iota((HOTS * CAP, 128), 0), CAP)
-    asked = jnp.sum(jnp.where(at_slot, asked, 0.0), axis=1, keepdims=True).astype(jnp.int32)
-    RTs[...] = (asked == iota((HOTS * CAP, ROWS), 1)).astype(BF16)
-    rs[...] = nn(RTs[...], ht[...].astype(BF16)).astype(BF16).reshape(HOTS, CAP, E)
-    each(HOTS, h, lambda p: send(rs.at[p], rr.at[h], ssem.at[3], rsem.at[3], p, t))
-    rr[h] = rs[h]
-
-    wait(hrv.at[pl.ds(0, HOTS - 1)], rsem.at[2])
-    zs[...] = tn(RTs[...], hrv[...].reshape(HOTS * CAP, E)).astype(BF16).reshape(TTS, CAP, E)
-    each(TTS, t, lambda p: send(zs.at[p], zr.at[t], ssem.at[4], rsem.at[4], h, p))
-    zr[t] = zs[t]
-
-    def from_plane(tp, _):
-        @pl.when(tp * 2 + k != t)
-        def _():
-            wait(G.at[k, ch, 0, rows16(rg), :], c1z_sem.at[tp])
-
-        return 0
-
-    lax.fori_loop(0, 8, from_plane, 0)
-    piece8 = G.at[k, ch, :, rows16(rg), :]
-    each(CHIPS, c, lambda p: send(piece8, piece8, ssem.at[5], rsem.at[5], p * 2 + k, t))
 
     def one_e(e, _):
         is_mid = iota((MIDS, CL), 0) == mi[...]
@@ -187,14 +180,6 @@
 
     lax.fori_loop(0, E3, one_e, 0)
 
-    wait(zr.at[pl.ds(0, TTS - 1)], rsem.at[4])
-    gs[...] = jnp.sum(zr[...].astype(F32), axis=0).astype(BF16)
-    each(TTS, t, lambda p: send(gs, gr.at[t], ssem.at[6], rsem.at[6], h, p))
-    gr[t] = gs[...]
-
-    wait(qr.at[pl.ds(0, CHIPS - 1)], rsem.at[5])
-    send(G.at[k], G.at[k], ssem.at[7], rsem.at[7], c * 2 + 1 - k, t)
-
     def back_lanes(kt, _):
         def back_e(e, acc):
             acc = list(acc)
@@ -234,6 +219,71 @@
 
     each(CHIPS, c, to_chip)
     qr[c] = qs[ch, :, rows16(rg), :]
+
+    wait(ids_r.at[pl.ds(0, HOTS - 1)], rsem.at[0])
+    asked = jnp.broadcast_to(ids_r[...], (HOTS, CAP, 128)).reshape(HOTS * CAP, 128)
+    at_slot = iota((HOTS * CAP, 128), 1) == lax.rem(iota((HOTS * CAP, 128), 0), CAP)
+    asked = jnp.sum(jnp.where(at_slot, asked, 0.0), axis=1, keepdims=True).astype(jnp.int32)
+    RTs[...] = (asked == iota((HOTS * CAP, ROWS), 1)).astype(BF16)
+    wait(hrv.at[pl.ds(0, HOTS - 1)], rsem.at[2])
+    zs[...] = tn(RTs[...], hrv[...].reshape(HOTS * CAP, E)).astype(BF16).reshape(TTS, CAP, E)
+    each(TTS, t, lambda p: send(zs.at[p], zr.at[t], ssem.at[4], rsem.at[4], h, p))
+    zr[t] = zs[t]
+
+    need(12)
+    rs[...] = nn(RTs[...], ht[...].astype(BF16)).astype(BF16).reshape(HOTS, CAP, E)
+    each(HOTS, h, lambda p: send(rs.at[p], rr.at[h], ssem.at[3], rsem.at[3], p, t))
+    rr[h] = rs[h]
+
+    def from_plane(tp, _):
+        @pl.when(tp * 2 + k != t)
+        def _():
+            wait(G.at[k, ch, 0, rows16(rg), :], c1z_sem.at[tp])
+
+        return 0
+
+    lax.fori_loop(0, 8, from_plane, 0)
+    piece8 = G.at[k, ch, :, rows16(rg), :]
+    each(CHIPS, c, lambda p: send(piece8, piece8, ssem.at[5], rsem.at[5], p * 2 + k, t))
+
+    wait(qr.at[pl.ds(0, CHIPS - 1)], rsem.at[9])
+    total = qr[0].astype(F32)
+    for i in range(1, CHIPS):
+        total = total + qr[i].astype(F32)
+    czs[...] = total.astype(BF16)
+
+    def to_owner(tp, _):
+        @pl.when(tp * 2 + k != t)
+        def _():
+            send(czs.at[tp], czr.at[t], ssem.at[10], c2z_sem.at[t], h, tp * 2 + k)
+
+        return 0
+
+    lax.fori_loop(0, 8, to_owner, 0)
+
+    wait(zr.at[pl.ds(0, TTS - 1)], rsem.at[4])
+    gs[...] = jnp.sum(zr[...].astype(F32), axis=0).astype(BF16)
+    each(TTS, t, lambda p: send(gs, gr.at[t], ssem.at[6], rsem.at[6], h, p))
+    gr[t] = gs[...]
+
+    wait(qr.at[pl.ds(0, CHIPS - 1)], rsem.at[5])
+    send(G.at[k], G.at[k], ssem.at[7], rsem.at[7], c * 2 + 1 - k, t)
+
+    @pl.when(mine)
+    def _():
+        czr[t] = czs[tp_me]
+
+        def from_tt(p, _):
+            @pl.when(p != t)
+            def _():
+                wait(czr.at[0], c2z_sem.at[p])
+
+            return 0
+
+        lax.fori_loop(0, TTS, from_tt, 0)
+        fs[...] = jnp.sum(czr[...].astype(F32), axis=0)
+        fr[c] = fs[...]
+        each(HOTS, h, lambda p: send(fs, fr.at[c], ssem.at[11], fr_sem.at[c], p, t))
 
     wait(G.at[0], rsem.at[7])
     for i in range(2):
@@ -267,43 +317,13 @@
     wait(rr.at[pl.ds(0, HOTS - 1)], rsem.at[3])
     pooled[...] = nt(cold_pick, rows_bf) + nn(SBs[...], rr[...].reshape(HOTS * CAP, E))
 
-    wait(qr.at[pl.ds(0, CHIPS - 1)], rsem.at[9])
-    total = qr[0].astype(F32)
-    for i in range(1, CHIPS):
-        total = total + qr[i].astype(F32)
-    czs[...] = total.astype(BF16)
-
-    def to_owner(tp, _):
-        @pl.when(tp * 2 + k != t)
-        def _():
-            send(czs.at[tp], czr.at[t], ssem.at[10], c2z_sem.at[t], h, tp * 2 + k)
-
-        return 0
-
-    lax.fori_loop(0, 8, to_owner, 0)
-
+    need(13)
     wait(gr.at[pl.ds(0, TTS - 1)], rsem.at[6])
     grad = gr[...].reshape(ROWS, E).astype(F32)
     accum = jnp.sum(jnp.where(eye, ha[...], 0.0), axis=1, keepdims=True)
     accum = accum + jnp.sum(grad * grad, axis=1, keepdims=True) * (1.0 / E)
     ntab[...] = ht[...] - 0.1 * grad / (jnp.sqrt(accum) + 1e-08)
     nacc[...] = jnp.sum(jnp.where(eye, accum, 0.0), axis=0, keepdims=True)
-
-    @pl.when(mine)
-    def _():
-        czr[t] = czs[tp_me]
-
-        def from_tt(p, _):
-            @pl.when(p != t)
-            def _():
-                wait(czr.at[0], c2z_sem.at[p])
-
-            return 0
-
-        lax.fori_loop(0, TTS, from_tt, 0)
-        fs[...] = jnp.sum(czr[...].astype(F32), axis=0)
-        fr[c] = fs[...]
-        each(HOTS, h, lambda p: send(fs, fr.at[c], ssem.at[11], fr_sem.at[c], p, t))
 
     def from_chip(p, _):
         @pl.when(p * 2 + lax.rem(t, 2) != h)
@@ -338,11 +358,20 @@
         wait(czr.at[pl.ds(0, 8)], ssem.at[10])
 
 
+def put_out(a_v, b_v, c_v, d_v, a_h, b_h, c_h, d_h, sem):
+    pairs = ((b_v, b_h), (d_v, d_h), (a_v, a_h), (c_v, c_h))
+    for i, (v, h) in enumerate(pairs):
+        pltpu.make_async_copy(v, h, sem.at[i]).start()
+    for i, (v, h) in enumerate(pairs):
+        pltpu.make_async_copy(v, h, sem.at[i]).wait()
+
+
 def local(
     hot_table, hot_accum, hot_owner, hot_row, hot_bag, cold_owner, first_index, mid_index, last_index, cold_bag,
     core_first, core_mid, core_last, bag_grads,
 ):
     vm = pl.BlockSpec(memory_space=pltpu.VMEM)
+    hbm = pl.BlockSpec(memory_space=pltpu.HBM)
     v = pltpu.VMEM
     outs = (
         jax.ShapeDtypeStruct((BAGS, E), F32),
@@ -351,6 +380,20 @@
         jax.ShapeDtypeStruct((SL, E), F32),
     )
     scratch = [
+        v((1, HL), jnp.int32),
+        v((1, HL), jnp.int32),
+        v((1, HL), jnp.int32),
+        v((BAGS, E), BF16),
+        v((1, CL), jnp.int32),
+        v((1, CL), jnp.int32),
+        v((1, CL), jnp.int32),
+        v((1, CL), jnp.int32),
+        v((1, CL), jnp.int32),
+        v((MIDS, RANK * E3), BF16),
+        v((SL, E), F32),
+        v((MIDS, RANK * E2 * RANK), BF16),
+        v((ROWS, E), F32),
+        v((1, ROWS), F32),
         v((HOTS, 1, 128), F32),
         v((HOTS, 1, 128), F32),
         v((HOTS, CAP, E), BF16),
@@ -383,23 +426,33 @@
         v((TTS, 16, 128), BF16),
         v((16, 128), F32),
         v((HOTS, 16, 128), F32),
+        pltpu.SemaphoreType.DMA((14,)),
         pltpu.SemaphoreType.DMA((12,)),
         pltpu.SemaphoreType.DMA((12,)),
         pltpu.SemaphoreType.DMA((8,)),
         pltpu.SemaphoreType.DMA((TTS,)),
         pltpu.SemaphoreType.DMA((CHIPS,)),
     ]
-    pooled, new_table, new_accum, new_first = pl.pallas_call(
+    operands = (
+        hot_owner.reshape(1, HL), hot_row, hot_bag, bag_grads, cold_owner.reshape(1, CL), first_index, cold_bag,
+        mid_index, last_index, core_last, core_first, core_mid, hot_table, hot_accum.reshape(1, ROWS),
+    )
+    results = pl.pallas_call(
         kernel,
         out_shape=outs,
-        in_specs=[vm] * 14,
+        in_specs=[hbm] * 14,
         out_specs=(vm,) * 4,
         scratch_shapes=scratch,
-        compiler_params=pltpu.CompilerParams(collective_id=0, has_side_effects=True),
-    )(
-        hot_table, hot_accum.reshape(1, ROWS), hot_owner, hot_row, hot_bag, cold_owner, first_index, mid_index,
-        last_index, cold_bag, core_first, core_mid, core_last, bag_grads,
-    )
+        compiler_params=pltpu.CompilerParams(collective_id=0, has_side_effects=True, vmem_limit_bytes=LIMIT),
+    )(*(pltpu.with_memory_space_constraint(a, pltpu.HBM) for a in operands))
+    pooled, new_table, new_accum, new_first = pl.pallas_call(
+        put_out,
+        out_shape=outs,
+        in_specs=[vm] * 4,
+        out_specs=(hbm,) * 4,
+        scratch_shapes=[pltpu.SemaphoreType.DMA((4,))],
+        compiler_params=pltpu.CompilerParams(vmem_limit_bytes=4 * 1024 * 1024),
+    )(*results)
     return pooled, new_table, new_accum.reshape(ROWS), new_first
 
 

time: 78.6 us -> 63.2 us (0.80)
  Pallas kernels: 71 us -> 62.4 us
  local copies, waits for them, and re-layouts: 6.74 us -> 0 us
    pallas_call x1 -> x2, Pallas kernels: 71 us -> 62.4 us  [the longest x1 61.6 us: local(): pl.pallas_call(kernel, out_shape=outs, in_specs=[hbm] * 14, out_specs=(vm...]
    unnamed x14 -> x0, local copies, waits for them, and re-layouts: 6.74 us -> none
where the time goes in v2:
time: 63.2 us; the launch traced here: 63.1 us
  Pallas kernels  62.4 us (99%)
  between operations  0.64 us (1%)
    pallas_call x1, Pallas kernels, local(): pl.pallas_call(kernel, out_shape=outs, in_specs=[hbm] * 14, out_specs=(vm...  61.6 us

profile of v2, /device:TPU:1, one launch (start us, length us, event | category | flops | bytes accessed | tf_op | source)
XLA Modules:
  0.0 63.1 jit_solution(6590809063464284002)
XLA Ops:
  0.6 61.6 %shard_map.165 = (f32[64,256]{1,0:T(8,128)S(1)}, f32[256,256]{1,0:T(8,128)S(1)}, f32[1,256]{1,0:T(1,128)S(1)}, f32[128,256]{1,0:T(8,128)S(1)}) custom-call(s32[1,256]{1,0:T(1,128)} %bitcast.5, s32[1,256]{1,0:T(1,128)} %hr_h.1, s32[1,256]{1,0:T(1,128)} %hb_h.1, bf16[64,256]{1,0:T(8,128)(2,1)} %bg_h.1, s32[1,512]{1,0:T(1,128)} %bitcast.4, s32[1,512]{1,0:T(1,128)} %fi_h.1, ...), custom_call_target="tpu_custom_call" | custom-call | tf_op jit(solution)/shard_map/pallas_call | solution.py:440
  62.3 0.8 %shard_map.166 = (f32[64,256]{1,0:T(8,128)}, f32[256,256]{1,0:T(8,128)}, f32[1,256]{1,0:T(1,128)}, f32[128,256]{1,0:T(8,128)}) custom-call(f32[64,256]{1,0:T(8,128)S(1)} %get-tuple-element.12.a_v, f32[256,256]{1,0:T(8,128)S(1)} %get-tuple-element.13.b_v, f32[1,256]{1,0:T(1,128)S(1)} %get-tuple-element.14.c_v, f32[128,256]{1,0:T(8,128)S(1)} %get-tuple-element.15.d_v), custom_call_target="tpu_custom_call" | custom-call | tf_op jit(solution)/shard_map/pallas_call | solution.py:448

commit v3 on v2

--- a/solution.py
+++ b/solution.py
@@ -90,16 +90,35 @@
     def rows16(r):
         return pl.ds(pl.multiple_of(r * 16, 16), 16)
 
-    def each(n, me, f):
-        def step(d, _):
-            f(lax.rem(me + d, n))
+    def far(i):
+        return 2 + 3 * i + 3 * (i // 2) + 2 * (i // 3)
+
+    def each_plane(f):
+        def step(i, _):
+            py = lax.rem(c // 4 + far(i // 8), 4)
+            px = lax.rem(c + far(lax.rem(i // 2, 4)), 4)
+            f((py * 4 + px) * 2 + lax.rem(k + i + 1, 2))
             return 0
 
-        lax.fori_loop(1, n, step, 0)
+        lax.fori_loop(0, HOTS - 1, step, 0)
+
+    def each_chip(f):
+        def step(i, _):
+            f(lax.rem(c // 4 + far(i // 4), 4) * 4 + lax.rem(c + far(lax.rem(i, 4)), 4))
+            return 0
+
+        lax.fori_loop(0, CHIPS - 1, step, 0)
+
+    def each_tt(f):
+        def step(i, _):
+            f(lax.rem(t + 8 + (i // 2) * (1 - 2 * lax.rem(i, 2)), TTS))
+            return 0
+
+        lax.fori_loop(1, TTS, step, 0)
 
     barrier = pltpu.get_barrier_semaphore()
-    each(HOTS, h, lambda p: pl.semaphore_signal(barrier, inc=1, device_id=(p, t), device_id_type=MESH))
-    each(TTS, t, lambda p: pl.semaphore_signal(barrier, inc=1, device_id=(h, p), device_id_type=MESH))
+    each_tt(lambda p: pl.semaphore_signal(barrier, inc=1, device_id=(h, p), device_id_type=MESH))
+    each_plane(lambda p: pl.semaphore_signal(barrier, inc=1, device_id=(p, t), device_id_type=MESH))
 
     need(0, 1, 2, 3)
     eye = iota((HL, HL), 0) == iota((HL, HL), 1)
@@ -115,26 +134,6 @@
     row_col = jnp.sum(jnp.where(eye, hr[...].astype(F32), 0.0), axis=1, keepdims=True)
     row_at = jnp.where(slot == iota((HL, 128), 1), row_col + 1.0, 0.0).astype(BF16)
     ids_s[...] = (tn(oh_owner.astype(BF16), row_at) - 1.0).reshape(HOTS, 1, 128)
-
-    need(10)
-    @pl.when(mine)
-    def _():
-        left = cf[rows16(rg), 0:128]
-        right = cf[rows16(rg), 128:256]
-        G[k, ch, tp_me, rows16(rg), :] = jnp.where(ch == 0, left, right).astype(BF16)
-
-    pl.semaphore_wait(barrier, HOTS - 1 + TTS - 1)
-
-    each(HOTS, h, lambda p: send(ids_s.at[p], ids_r.at[h], ssem.at[0], rsem.at[0], p, t))
-
-    @pl.when(mine)
-    def _():
-        piece = G.at[k, ch, tp_me, rows16(rg), :]
-        each(TTS, t, lambda p: send(piece, piece, ssem.at[1], c1z_sem.at[tp_me], h, p))
-
-    each(HOTS, h, lambda p: send(hs.at[p], hrv.at[h], ssem.at[2], rsem.at[2], p, t))
-    ids_r[h] = ids_s[h]
-    hrv[h] = hs[h]
 
     need(4, 5, 6, 7, 8, 9)
     owner = co[...]
@@ -154,17 +153,39 @@
         for e in range(E3):
             LT[e, :, n * 128 : (n + 1) * 128] = M2[n, pl.ds(e, RANK, stride=E3), :]
 
+    need(10)
+    @pl.when(mine)
+    def _():
+        left = cf[rows16(rg), 0:128]
+        right = cf[rows16(rg), 128:256]
+        G[k, ch, tp_me, rows16(rg), :] = jnp.where(ch == 0, left, right).astype(BF16)
+
     need(11)
-    def turn(j, _):
-        blk = mid[:, pl.ds(pl.multiple_of(j * 128, 128), 128)].astype(F32).T
-        parts = blk.reshape(4, 2, 16, MIDS)
-        wide = jnp.concatenate([parts[:, 0], parts[:, 1]], axis=-1).reshape(64, 128)
-        T[pl.ds(pl.multiple_of(j * 64, 64), 64), :] = wide
-        return 0
-
-    lax.fori_loop(0, 64, turn, 0)
+    def turn(g, _):
+        for u in range(8):
+            j = g * 8 + u
+            blk = mid[:, pl.ds(pl.multiple_of(j * 128, 128), 128)].astype(F32).T
+            parts = blk.reshape(4, 2, 16, MIDS)
+            wide = jnp.concatenate([parts[:, 0], parts[:, 1]], axis=-1).reshape(64, 128)
+            T[pl.ds(pl.multiple_of(j * 64, 64), 64), :] = wide
+        return 0
+
+    lax.fori_loop(0, 8, turn, 0)
     for n in range(16):
         LHS[:, n * 128 : (n + 1) * 128] = T[pl.ds(n, 256, stride=16), :].astype(BF16)
+
+    pl.semaphore_wait(barrier, HOTS - 1 + TTS - 1)
+
+    each_plane(lambda p: send(ids_s.at[p], ids_r.at[h], ssem.at[0], rsem.at[0], p, t))
+
+    @pl.when(mine)
+    def _():
+        piece = G.at[k, ch, tp_me, rows16(rg), :]
+        each_tt(lambda p: send(piece, piece, ssem.at[1], c1z_sem.at[tp_me], h, p))
+
+    each_plane(lambda p: send(hs.at[p], hrv.at[h], ssem.at[2], rsem.at[2], p, t))
+    ids_r[h] = ids_s[h]
+    hrv[h] = hs[h]
 
     def one_e(e, _):
         is_mid = iota((MIDS, CL), 0) == mi[...]
@@ -202,37 +223,38 @@
     def half(which):
         return OHS[pl.ds(pl.multiple_of(which * 1024, 1024), 1024), :]
 
-    other = nt(half(1 - k), terms).astype(BF16)
-    dsn[0] = other[:, :128].reshape(8, SL, 128)
-    dsn[1] = other[:, 128:].reshape(8, SL, 128)
-    send(dsn, dr, ssem.at[8], rsem.at[8], c * 2 + 1 - k, t)
+    for i in range(2):
+        dsn[i] = nt(half(1 - k), terms[i * 128 : (i + 1) * 128]).astype(BF16).reshape(8, SL, 128)
+        send(dsn.at[i], dr.at[i], ssem.at[8], rsem.at[8 + 6 * i], c * 2 + 1 - k, t)
     pown[...] = nt(half(k), terms)
-
-    wait(dr, rsem.at[8])
-    for i in range(2):
-        mine_f = pown[:, i * 128 : (i + 1) * 128].reshape(8, SL, 128)
-        qs[i] = (mine_f + dr[i].astype(F32)).astype(BF16)
-
-    def to_chip(p):
-        src = qs.at[lax.rem(p, 2), :, rows16(p // 2), :]
-        send(src, qr.at[c], ssem.at[9], rsem.at[9], p * 2 + k, t)
-
-    each(CHIPS, c, to_chip)
-    qr[c] = qs[ch, :, rows16(rg), :]
 
     wait(ids_r.at[pl.ds(0, HOTS - 1)], rsem.at[0])
     asked = jnp.broadcast_to(ids_r[...], (HOTS, CAP, 128)).reshape(HOTS * CAP, 128)
     at_slot = iota((HOTS * CAP, 128), 1) == lax.rem(iota((HOTS * CAP, 128), 0), CAP)
     asked = jnp.sum(jnp.where(at_slot, asked, 0.0), axis=1, keepdims=True).astype(jnp.int32)
     RTs[...] = (asked == iota((HOTS * CAP, ROWS), 1)).astype(BF16)
+    for i in range(2):
+        wait(dr.at[i], rsem.at[8 + 6 * i])
+        mine_f = pown[:, i * 128 : (i + 1) * 128].reshape(8, SL, 128)
+        qs[i] = (mine_f + dr[i].astype(F32)).astype(BF16)
+
+    def to_chip(p):
+        src = qs.at[lax.rem(p, 2), :, rows16(p // 2), :]
+        send(src, qr.at[c], ssem.at[9], rsem.at[9], p * 2 + k, t)
+
+    each_chip(to_chip)
+    qr[c] = qs[ch, :, rows16(rg), :]
+
     wait(hrv.at[pl.ds(0, HOTS - 1)], rsem.at[2])
-    zs[...] = tn(RTs[...], hrv[...].reshape(HOTS * CAP, E)).astype(BF16).reshape(TTS, CAP, E)
-    each(TTS, t, lambda p: send(zs.at[p], zr.at[t], ssem.at[4], rsem.at[4], h, p))
-    zr[t] = zs[t]
+    part = tn(RTs[...], hrv[...].reshape(HOTS * CAP, E)).astype(BF16)
+    for i in range(2):
+        zs[i] = part[:, i * 128 : (i + 1) * 128].reshape(TTS, CAP, 128)
+        each_tt(lambda p: send(zs.at[i, p], zr.at[i, t], ssem.at[4], rsem.at[4 + 8 * i], h, p))
+        zr[i, t] = zs[i, t]
 
     need(12)
     rs[...] = nn(RTs[...], ht[...].astype(BF16)).astype(BF16).reshape(HOTS, CAP, E)
-    each(HOTS, h, lambda p: send(rs.at[p], rr.at[h], ssem.at[3], rsem.at[3], p, t))
+    each_plane(lambda p: send(rs.at[p], rr.at[h], ssem.at[3], rsem.at[3], p, t))
     rr[h] = rs[h]
 
     def from_plane(tp, _):
@@ -244,7 +266,12 @@
 
     lax.fori_loop(0, 8, from_plane, 0)
     piece8 = G.at[k, ch, :, rows16(rg), :]
-    each(CHIPS, c, lambda p: send(piece8, piece8, ssem.at[5], rsem.at[5], p * 2 + k, t))
+    each_chip(lambda p: send(piece8, piece8, ssem.at[5], rsem.at[5], p * 2 + k, t))
+
+    wait(zr.at[0, pl.ds(0, TTS - 1)], rsem.at[4])
+    gs[0] = jnp.sum(zr[0].astype(F32), axis=0).astype(BF16)
+    each_tt(lambda p: send(gs.at[0], gr.at[0, t], ssem.at[6], rsem.at[6], h, p))
+    gr[0, t] = gs[0]
 
     wait(qr.at[pl.ds(0, CHIPS - 1)], rsem.at[9])
     total = qr[0].astype(F32)
@@ -261,10 +288,10 @@
 
     lax.fori_loop(0, 8, to_owner, 0)
 
-    wait(zr.at[pl.ds(0, TTS - 1)], rsem.at[4])
-    gs[...] = jnp.sum(zr[...].astype(F32), axis=0).astype(BF16)
-    each(TTS, t, lambda p: send(gs, gr.at[t], ssem.at[6], rsem.at[6], h, p))
-    gr[t] = gs[...]
+    wait(zr.at[1, pl.ds(0, TTS - 1)], rsem.at[12])
+    gs[1] = jnp.sum(zr[1].astype(F32), axis=0).astype(BF16)
+    each_tt(lambda p: send(gs.at[1], gr.at[1, t], ssem.at[6], rsem.at[13], h, p))
+    gr[1, t] = gs[1]
 
     wait(qr.at[pl.ds(0, CHIPS - 1)], rsem.at[5])
     send(G.at[k], G.at[k], ssem.at[7], rsem.at[7], c * 2 + 1 - k, t)
@@ -283,7 +310,7 @@
         lax.fori_loop(0, TTS, from_tt, 0)
         fs[...] = jnp.sum(czr[...].astype(F32), axis=0)
         fr[c] = fs[...]
-        each(HOTS, h, lambda p: send(fs, fr.at[c], ssem.at[11], fr_sem.at[c], p, t))
+        each_plane(lambda p: send(fs, fr.at[c], ssem.at[11], fr_sem.at[c], p, t))
 
     wait(G.at[0], rsem.at[7])
     for i in range(2):
@@ -318,8 +345,9 @@
     pooled[...] = nt(cold_pick, rows_bf) + nn(SBs[...], rr[...].reshape(HOTS * CAP, E))
 
     need(13)
-    wait(gr.at[pl.ds(0, TTS - 1)], rsem.at[6])
-    grad = gr[...].reshape(ROWS, E).astype(F32)
+    wait(gr.at[0, pl.ds(0, TTS - 1)], rsem.at[6])
+    wait(gr.at[1, pl.ds(0, TTS - 1)], rsem.at[13])
+    grad = jnp.concatenate([gr[0].reshape(ROWS, 128), gr[1].reshape(ROWS, 128)], axis=1).astype(F32)
     accum = jnp.sum(jnp.where(eye, ha[...], 0.0), axis=1, keepdims=True)
     accum = accum + jnp.sum(grad * grad, axis=1, keepdims=True) * (1.0 / E)
     ntab[...] = ht[...] - 0.1 * grad / (jnp.sqrt(accum) + 1e-08)
@@ -340,9 +368,9 @@
     wait(ids_r.at[pl.ds(0, HOTS - 1)], ssem.at[0])
     wait(hrv.at[pl.ds(0, HOTS - 1)], ssem.at[2])
     wait(rr.at[pl.ds(0, HOTS - 1)], ssem.at[3])
-    wait(zr.at[pl.ds(0, TTS - 1)], ssem.at[4])
+    wait(zr.at[:, pl.ds(0, TTS - 1)], ssem.at[4])
     wait(qr.at[pl.ds(0, CHIPS - 1)], ssem.at[5])
-    wait(gr.at[pl.ds(0, TTS - 1)], ssem.at[6])
+    wait(gr.at[:, pl.ds(0, TTS - 1)], ssem.at[6])
     wait(G.at[0], ssem.at[7])
     wait(dsn, ssem.at[8])
     wait(qr.at[pl.ds(0, CHIPS - 1)], ssem.at[9])
@@ -400,10 +428,10 @@
         v((HOTS, CAP, E), BF16),
         v((HOTS, CAP, E), BF16),
         v((HOTS, CAP, E), BF16),
-        v((TTS, CAP, E), BF16),
-        v((TTS, CAP, E), BF16),
-        v((CAP, E), BF16),
-        v((TTS, CAP, E), BF16),
+        v((2, TTS, CAP, 128), BF16),
+        v((2, TTS, CAP, 128), BF16),
+        v((2, CAP, 128), BF16),
+        v((2, TTS, CAP, 128), BF16),
         v((2, 2, 8, SL, 128), BF16),
         v((4096, 128), F32),
         v((256, 2048), BF16),
@@ -427,8 +455,8 @@
         v((16, 128), F32),
         v((HOTS, 16, 128), F32),
         pltpu.SemaphoreType.DMA((14,)),
-        pltpu.SemaphoreType.DMA((12,)),
-        pltpu.SemaphoreType.DMA((12,)),
+        pltpu.SemaphoreType.DMA((16,)),
+        pltpu.SemaphoreType.DMA((16,)),
         pltpu.SemaphoreType.DMA((8,)),
         pltpu.SemaphoreType.DMA((TTS,)),
         pltpu.SemaphoreType.DMA((CHIPS,)),

time: 63.2 us -> 54.8 us (0.87)
  Pallas kernels: 62.4 us -> 54 us
    pallas_call x1, Pallas kernels: 61.6 us -> 53.2 us  [local(): pl.pallas_call(kernel, out_shape=outs, in_specs=[hbm] * 14, out_specs=(vm...]
where the time goes in v3:
time: 54.8 us; the launch traced here: 54.6 us
  Pallas kernels  54 us (99%)
  between operations  0.64 us (1%)
    pallas_call x1, Pallas kernels, local(): pl.pallas_call(kernel, out_shape=outs, in_specs=[hbm] * 14, out_specs=(vm...  53.2 us

profile of v3, /device:TPU:1, one launch (start us, length us, event | category | flops | bytes accessed | tf_op | source)
XLA Modules:
  0.0 54.6 jit_solution(11814768086992736805)
XLA Ops:
  0.6 53.2 %shard_map.165 = (f32[64,256]{1,0:T(8,128)S(1)}, f32[256,256]{1,0:T(8,128)S(1)}, f32[1,256]{1,0:T(1,128)S(1)}, f32[128,256]{1,0:T(8,128)S(1)}) custom-call(s32[1,256]{1,0:T(1,128)} %bitcast.5, s32[1,256]{1,0:T(1,128)} %hr_h.1, s32[1,256]{1,0:T(1,128)} %hb_h.1, bf16[64,256]{1,0:T(8,128)(2,1)} %bg_h.1, s32[1,512]{1,0:T(1,128)} %bitcast.4, s32[1,512]{1,0:T(1,128)} %fi_h.1, ...), custom_call_target="tpu_custom_call" | custom-call | tf_op jit(solution)/shard_map/pallas_call | solution.py:468
  53.8 0.8 %shard_map.166 = (f32[64,256]{1,0:T(8,128)}, f32[256,256]{1,0:T(8,128)}, f32[1,256]{1,0:T(1,128)}, f32[128,256]{1,0:T(8,128)}) custom-call(f32[64,256]{1,0:T(8,128)S(1)} %get-tuple-element.12.a_v, f32[256,256]{1,0:T(8,128)S(1)} %get-tuple-element.13.b_v, f32[1,256]{1,0:T(1,128)S(1)} %get-tuple-element.14.c_v, f32[128,256]{1,0:T(8,128)S(1)} %get-tuple-element.15.d_v), custom_call_target="tpu_custom_call" | custom-call | tf_op jit(solution)/shard_map/pallas_call | solution.py:476
